TPU v7x, 32 devices: a whole 2x2x4 slice. The times are simulated.
32 devices in a mesh: grp: 4 (over x, core), dev: 8 (over z, y).
Axes of the slice: x: 2, y: 2, z: 4, core: 2. Of those that a mesh axis runs over, the one named last changes fastest.
Arguments:
- points: bfloat16 [65536, 1024], P(('grp', 'dev')), may hold values from -6 to 6
- blocks: int32 [65536, 1], P(('grp', 'dev')), may hold values from 0 to 63; in each aligned block of 2048 rows (0 to 2047, 2048 to 4095, ...) at most 64 rows name the same one
- finals: int32 [65536], P(('grp', 'dev')), may hold values from 0 to 255
- centroids: bfloat16 [16384, 1024], P('dev'), may hold values from -6 to 6
Outputs:
- distances: bfloat16 [65536, 256], P(('grp', 'dev'))
- refreshed_centroids: float32 [16384, 1024], P('dev', 'grp')
Inputs may be any that keep to these rules, and one draw needn't show every extreme that they name: `blocks`: among the 2048 rows of one device no block is named by more than 64 rows, and some block by exactly 64. Block b is held by index b // 8 of dev. The point's centroid is row 256 * blocks + finals of centroids.
All inputs are finite; a program needn't handle non-finite values.
Results may differ from a plain program's by a relative error of at most 0.008.
Values may be sent and summed in bfloat16 or wider, within the bound.
A program may use at most 128 MiB of HBM per device.

v0:
```python
import functools

import jax
import jax.numpy as jnp
from jax import lax
from jax.experimental import pallas as pl
from jax.experimental.pallas import tpu as pltpu
from jax.sharding import PartitionSpec as P

BS = 256
MESH = pl.DeviceIdType.MESH
F32, BF16 = jnp.float32, jnp.bfloat16


def kernel(
    n_grp, n_dev, owned, depth,
    place_row, block_row, final_row, points_hbm, cent_hbm, cn_own,
    distances, col_sums, counts_out,
    points, cent, slot_row, slot_col, out, recv, tgt_out, tgt_in, tgt_col, others, cn_oth,
    part, pair_in, x_in, fin, mid_in, dist, ret,
    cnt, cnt_in, cnt_fin, cnt_mid,
    s_pts, r_pts, s_tgt, r_tgt, s_cen, r_cen, s_fwd, r_fwd, s_cn, r_cn,
    s_pair, r_pair, s_x, r_x, s_mid, r_mid, s_cnt, r_cnt, s_cm, r_cm, s_ret, r_ret, l_sem, in_sem,
):
    team = n_dev // 2
    n_x = n_grp // 2
    g, d = lax.axis_index("grp"), lax.axis_index("dev")
    x, c = g // 2, g % 2
    half, me = d // team, d % team
    npts, width = points.shape
    rows = cent.shape[0]
    share = width // n_grp
    piece = rows // n_grp
    n_cut = 2
    pc = piece // n_cut
    per = owned * depth
    tile = min(256, per)
    nb = tile // depth

    def to(gg, dd):
        return {"grp": gg, "dev": dd}

    def mate(o):
        return half * team + (me + o) % team

    def copy(src, dst, ss, rs, dev):
        return pltpu.make_async_remote_copy(
            src_ref=src, dst_ref=dst, send_sem=ss, recv_sem=rs, device_id=dev, device_id_type=MESH
        )

    load_points = pltpu.make_async_copy(points_hbm, points, in_sem.at[0])
    load_cent = pltpu.make_async_copy(cent_hbm, cent, in_sem.at[1])
    load_points.start()

    swap = to(g, (d + team) % n_dev)
    barrier = pltpu.get_barrier_semaphore()
    peers = [to(g, mate(o)) for o in range(1, team)] + [swap]
    peers += [to((g + o) % n_grp, d) for o in range(1, n_grp)]
    for p in peers:
        pl.semaphore_signal(barrier, inc=1, device_id=p, device_id_type=MESH)
    pl.semaphore_wait(barrier, len(peers))

    def span(gg, j):
        return pl.ds(pl.multiple_of(gg * piece + j * pc, pc), pc)

    cen = [copy(cent_hbm.at[span(g, j)], others.at[span(g, j)], s_cen.at[j], r_cen.at[j], swap) for j in range(n_cut)]
    cnc = copy(cn_own, cn_oth, s_cn.at[0], r_cn.at[0], swap)
    for j in range(n_cut):
        cen[j].start()
    cnc.start()
    load_cent.start()

    n_blocks = owned * n_dev
    step = min(256, npts)
    before = (
        lax.broadcasted_iota(jnp.int32, (step, step), 0) < lax.broadcasted_iota(jnp.int32, (step, step), 1)
    ).astype(BF16)
    seen = jnp.zeros((n_blocks, 1), F32)
    for t in range(npts // step):
        here = slice(t * step, (t + 1) * step)
        member = (lax.broadcasted_iota(jnp.int32, (n_blocks, step), 0) == block_row[:, here]).astype(F32)
        prior = jnp.dot(member.astype(BF16), before, preferred_element_type=F32) + seen
        rank = jnp.sum(member * prior, axis=0, keepdims=True)
        seen = seen + jnp.sum(member, axis=1, keepdims=True)
        slot = place_row[:, here] * depth + rank.astype(jnp.int32)
        slot_row[:, here] = slot
        slot_col[here, :] = jnp.transpose(jnp.broadcast_to(slot.astype(F32), (8, step)))
    load_points.wait()

    fwd = [
        copy(others.at[span(g, j)], others.at[span(g, j)], s_fwd.at[j, o], r_fwd.at[j, o], to((g + o) % n_grp, d))
        for j in range(n_cut)
        for o in range(1, n_grp)
    ]

    def packed(h, who, t):
        base = ((who * 2 + h) * owned) * depth + t * tile
        hot = (lax.broadcasted_iota(jnp.int32, (tile, npts), 0) + base == slot_row[...]).astype(BF16)
        pts = jnp.dot(hot, points[...], preferred_element_type=F32).astype(BF16)
        tg = lax.dot_general(final_row[...], hot, (((1,), (1,)), ((), ())), preferred_element_type=F32)
        return pts.reshape(nb, depth, width), tg

    mine = pl.ds(pl.multiple_of(me * depth, depth), depth)
    pts_c, tgt_c = {}, {}
    for h in (1, 0):
        for o in range(1, team):
            pts_c[h, o] = copy(out.at[h, o - 1], recv.at[h, :, mine], s_pts.at[h, o], r_pts.at[h, o], to(g, mate(o)))
            tgt_c[h, o] = copy(tgt_out.at[h, o - 1], tgt_in.at[h, o - 1], s_tgt.at[h, o], r_tgt.at[h, o], to(g, mate(o)))

    def pack_all(h):
        for o in list(range(team // 2, team)) + list(range(1, team // 2)):
            for t in range(per // tile):
                pts, tg = packed(h, (me + o) % team, t)
                out[h, o - 1, t * nb : (t + 1) * nb] = pts
                tgt_out[h, o - 1, :, t * tile : (t + 1) * tile] = tg
            pts_c[h, o].start()
            tgt_c[h, o].start()

    def put_targets(h, src, tg):
        col = jnp.transpose(tg)
        tgt_col[h, :, pl.ds(pl.multiple_of(src * depth, depth), depth), :] = col.reshape(-1, depth, 8)

    def pack_own(h):
        for t in range(per // tile):
            pts, tg = packed(h, me, t)
            recv[h, t * nb : (t + 1) * nb, mine] = pts
            tgt_col[h, t * nb : (t + 1) * nb, mine, :] = jnp.transpose(tg).reshape(nb, depth, 8)

    def forward(j):
        cen[j].wait_recv()
        for o in range(1, n_grp):
            fwd[j * (n_grp - 1) + o - 1].start()

    pack_all(1)
    pack_own(1)
    forward(0)
    pack_all(0)
    pack_own(0)
    for j in range(1, n_cut):
        forward(j)

    pair_c = {
        (h, xx): copy(part.at[h, xx * 2 + 1 - c], pair_in.at[h, xx], s_pair.at[h, xx], r_pair.at[h, xx], to(x * 2 + 1 - c, d))
        for h in (1, 0)
        for xx in range(n_x)
    }
    x_c = {
        (h, o): copy(part.at[h, (x + o) % n_x * 2 + c], x_in.at[h, o - 1], s_x.at[h, o], r_x.at[h, o], to((x + o) % n_x * 2 + c, d))
        for h in (1, 0)
        for o in range(1, n_x)
    }
    ret_c = {
        (h, o): copy(dist.at[h, :, pl.ds(pl.multiple_of((me + o) % team * depth, depth), depth)],
                     ret.at[h, me], s_ret.at[h, o], r_ret.at[h, o], to(g, mate(o)))
        for h in (1, 0)
        for o in range(1, team)
    }
    cnt_c = {
        o: copy(cnt, cnt_in.at[o - 1], s_cnt.at[o], r_cnt.at[o], to((g + o) % n_grp, d)) for o in range(1, n_grp)
    }
    mid_c = copy(fin, mid_in, s_mid.at[0], r_mid.at[0], swap)
    cm_c = copy(cnt_fin.at[1], cnt_mid, s_cm.at[0], r_cm.at[0], swap)

    def sums(h):
        for o in range(1, team):
            pts_c[h, o].wait_recv()
            tgt_c[h, o].wait_recv()
            put_targets(h, (me + team - o) % team, tgt_in[h, o - 1])

        @pl.loop(0, owned)
        def _(b):
            want = tgt_col[h, b][:, 0:1].astype(jnp.int32) - 1
            hot = (lax.broadcasted_iota(jnp.int32, (team * depth, BS), 1) == want).astype(F32)
            cnt[h, pl.ds(b, 1), :] = jnp.sum(hot, axis=0, keepdims=True)
            s = lax.dot_general(hot.astype(BF16), recv[h, b], (((0,), (0,)), ((), ())), preferred_element_type=F32)
            s = s.astype(BF16)
            here = pl.ds(pl.multiple_of(b * BS, BS), BS)
            for k in range(n_grp):
                part[h, k, here, :] = s[:, k * share : (k + 1) * share]

        for xx in range(n_x):
            pair_c[h, xx].start()

    def pair(h):
        for xx in range(n_x):
            pair_c[h, xx].wait_recv()
        for o in list(range(1, n_x)) + [0]:
            xx = (x + o) % n_x

            @pl.loop(0, rows // BS)
            def _(b):
                here = pl.ds(pl.multiple_of(b * BS, BS), BS)
                both = part[h, xx * 2 + c, here, :].astype(F32) + pair_in[h, xx, here, :].astype(F32)
                part[h, xx * 2 + c, here, :] = both.astype(BF16)

            if o:
                x_c[h, o].start()

    def dists(h):
        table, norm = (cent, cn_own) if h == 0 else (others, cn_oth)

        @pl.loop(0, owned)
        def _(b):
            pts = recv[h, b]
            tab = table[pl.ds(pl.multiple_of(b * BS, BS), BS), :]
            cross = lax.dot_general(pts, tab, (((1,), (1,)), ((), ())), preferred_element_type=F32)
            wide = pts.astype(F32)
            rn = jnp.sum(wide * wide, axis=1, keepdims=True)
            dist[h, b] = ((rn - 2.0 * cross + norm[pl.ds(b, 1), :]) / width).astype(BF16)

        for o in range(1, team):
            ret_c[h, o].start()
        own = pltpu.make_async_copy(dist.at[h, :, mine], ret.at[h, me], l_sem.at[h])
        own.start()
        own.wait()

    def total(h, here):
        acc = part[h, x * 2 + c, here, :].astype(F32)
        for o in range(1, n_x):
            acc += x_in[h, o - 1, here, :].astype(F32)
        return acc

    load_cent.wait()
    sums(1)
    pair(1)
    for j in range(n_cut):
        for o in range(1, n_grp):
            fwd[j * (n_grp - 1) + o - 1].wait_recv()
    cnc.wait_recv()
    dists(1)
    for o in range(1, n_x):
        x_c[1, o].wait_recv()

    @pl.loop(0, rows // BS)
    def _(b):
        here = pl.ds(pl.multiple_of(b * BS, BS), BS)
        fin[here, :] = total(1, here).astype(BF16)

    mid_c.start()
    sums(0)
    for o in range(1, n_grp):
        cnt_c[o].start()
    dists(0)
    pair(0)
    for o in range(1, n_grp):
        cnt_c[o].wait_recv()
    acc = cnt[...]
    for o in range(1, n_grp):
        acc += cnt_in[o - 1]
    cnt_fin[...] = acc
    cm_c.start()
    ptile = min(256, npts)

    def gather(h):
        for o in range(1, team):
            ret_c[h, o].wait_recv()

        @pl.loop(0, npts // ptile)
        def _(t):
            here = pl.ds(pl.multiple_of(t * ptile, ptile), ptile)
            where = slot_col[here, 0:1].astype(jnp.int32)
            acc = jnp.zeros((ptile, BS), F32)
            for s in range(team):
                base = (s * 2 + h) * per
                hot = (lax.broadcasted_iota(jnp.int32, (ptile, per), 1) + base == where).astype(BF16)
                acc += jnp.dot(hot, ret[h, s].reshape(per, BS), preferred_element_type=F32)
            if h == 0:
                acc += distances[here, :].astype(F32)
            distances[here, :] = acc.astype(BF16)

    gather(1)
    gather(0)
    for o in range(1, n_x):
        x_c[0, o].wait_recv()
    mid_c.wait_recv()

    @pl.loop(0, rows // BS)
    def _(b):
        here = pl.ds(pl.multiple_of(b * BS, BS), BS)
        col_sums[here, :] = total(0, here) + mid_in[here, :].astype(F32)

    cm_c.wait_recv()
    counts_out[...] = cnt_fin[0] + cnt_mid[...]

    for q in cen + [cnc] + fwd + [mid_c, cm_c]:
        q.wait_send()
    for group in (pts_c, tgt_c, pair_c, x_c, ret_c, cnt_c):
        for q in group.values():
            q.wait_send()


def shards(points, blocks, finals, centroids):
    n_dev = lax.axis_size("dev")
    n_grp = lax.axis_size("grp")
    team = n_dev // 2
    half = lax.axis_index("dev") // team
    npoints, width = points.shape
    rows = centroids.shape[0]
    owned = rows // BS
    nblocks = owned * n_dev
    depth = 2 * npoints // nblocks
    share = width // n_grp
    piece = rows // n_grp
    n_x = n_grp // 2
    per = owned * depth

    block_ids = blocks[:, 0]
    holder = block_ids // owned
    other = (holder // team) ^ half
    place = ((holder % team) * 2 + other) * owned + block_ids % owned
    final_row = jnp.broadcast_to((finals + 1).astype(BF16)[None, :], (8, npoints))
    cn = jnp.sum(jnp.square(centroids.astype(F32)), axis=-1).reshape(owned, BS)

    dma = pltpu.SemaphoreType.DMA
    vm = pltpu.VMEM
    distances, col_sums, counts = pl.pallas_call(
        functools.partial(kernel, n_grp, n_dev, owned, depth),
        out_shape=(
            jax.ShapeDtypeStruct((npoints, BS), BF16),
            jax.ShapeDtypeStruct((rows, share), F32),
            jax.ShapeDtypeStruct((owned, BS), F32),
        ),
        in_specs=[pl.BlockSpec(memory_space=vm)] * 3
        + [pl.BlockSpec(memory_space=pl.ANY)] * 2
        + [pl.BlockSpec(memory_space=vm)],
        out_specs=(pl.BlockSpec(memory_space=vm),) * 3,
        scratch_shapes=[
            vm((npoints, width), BF16),
            vm((rows, width), BF16),
            vm((1, npoints), jnp.int32),
            vm((npoints, 8), F32),
            vm((2, team - 1, owned, depth, width), BF16),
            vm((2, owned, team * depth, width), BF16),
            vm((2, team - 1, 8, per), F32),
            vm((2, team - 1, 8, per), F32),
            vm((2, owned, team * depth, 8), F32),
            vm((rows, width), BF16),
            vm((owned, BS), F32),
            vm((2, n_grp, rows, share), BF16),
            vm((2, n_x, rows, share), BF16),
            vm((2, max(n_x - 1, 1), rows, share), BF16),
            vm((rows, share), BF16),
            vm((rows, share), BF16),
            vm((2, owned, team * depth, BS), BF16),
            vm((2, team, owned, depth, BS), BF16),
            vm((2, owned, BS), F32),
            vm((n_grp - 1, 2, owned, BS), F32),
            vm((2, owned, BS), F32),
            vm((owned, BS), F32),
            dma((2, team)), dma((2, team)), dma((2, team)), dma((2, team)),
            dma((2,)), dma((2,)), dma((2, n_grp)), dma((2, n_grp)), dma((1,)), dma((1,)),
            dma((2, n_x)), dma((2, n_x)), dma((2, n_x)), dma((2, n_x)),
            dma((1,)), dma((1,)), dma((n_grp,)), dma((n_grp,)), dma((1,)), dma((1,)),
            dma((2, team)), dma((2, team)), dma((2,)), dma((2,)),
        ],
        compiler_params=pltpu.CompilerParams(
            collective_id=0, has_side_effects=True, vmem_limit_bytes=67_000_000
        ),
    )(place[None, :], block_ids[None, :], final_row, points, centroids, cn)

    own_cols = lax.dynamic_slice_in_dim(centroids, lax.axis_index("grp") * share, share, 1).astype(F32)
    refreshed_centroids = (col_sums + own_cols) / (counts.reshape(rows) + 1.0)[:, None]
    return (distances, refreshed_centroids)


def solution(mesh):
    placed = (P(("grp", "dev"), None), P(("grp", "dev"), None), P(("grp", "dev")), P("dev", None))
    return jax.shard_map(
        shards,
        mesh=mesh,
        in_specs=placed,
        out_specs=(P(("grp", "dev"), None), P("dev", "grp")),
        check_vma=False,
    )
```

profile of v0, /device:TPU:0, one launch (start us, length us, event | category | flops | bytes accessed | tf_op | source)
XLA Modules:
  0.0 195.7 jit_solution(10313147875242247856)
XLA Ops:
  0.6 0.7 add_convert_fusion
  1.3 1.4 fusion.place_row
  2.8 3.1 %multiply_reduce_fusion = f32[2048]{0:T(1024)S(1)} fusion(bf16[2048,1024]{1,0:T(8,128)(2,1)} %cent_hbm.1), kind=kLoop, calls=%fused_computation | loop fusion | flops 6289408 | bytes 4202496 | tf_op jit(solution)/shard_map/reduce_sum | solution.py:312
  5.8 0.6 reshape.190.cn_own
  6.4 0.6 broadcast_in_dim.2.final_row
  7.1 183.3 %shard_map.59 = (bf16[2048,256]{1,0:T(8,128)(2,1)}, f32[2048,256]{1,0:T(8,128)}, f32[8,256]{1,0:T(8,128)}) custom-call(s32[1,2048]{1,0:T(1,128)} %fusion.place_row, s32[1,2048]{1,0:T(1,128)} %bitcast.5, bf16[8,2048]{1,0:T(8,128)(2,1)} %broadcast_in_dim.2.final_row, bf16[2048,1024]{1,0:T(8,128)(2,1)} %points_hbm.1, bf16[2048,1024]{1,0:T(8,128)(2,1)} %cent_hbm.1, ...), custom_call_target="tpu_custom_call" | custom-call | tf_op jit(solution)/shard_map/pallas_call | solution.py:316
  190.4 0.7 add_bitcast_fusion
  191.1 0.0 copy-start
  191.1 3.6 %add_divide_fusion = f32[2048,256]{1,0:T(8,128)} fusion(f32[2048,256]{1,0:T(8,128)} %get-tuple-element.6, f32[2048]{0:T(1024)S(1)} %bitcast.6, bf16[2048,1024]{1,0:T(8,128)(2,1)} %cent_hbm.1, s32[]{:T(128)S(6)} %select_n.59), kind=kLoop, calls=%fused_computation.1 | loop fusion | flops 1572864 | bytes 5251076 | tf_op jit(solution)/shard_map/div | solution.py:362
  194.7 0.0 copy-done
  194.7 1.0 copy.8
  (1 shorter events, 0.0 us)
Async XLA Ops:
  191.1 3.6 %copy-start = (bf16[2048,256]{1,0:T(8,128)(2,1)S(1)}, bf16[2048,256]{1,0:T(8,128)(2,1)}, u32[]{:S(2)}) copy-start(bf16[2048,256]{1,0:T(8,128)(2,1)} %get-tuple-element.10) | copy-start | bytes 3145732
where the time goes:
time: 196 us
  Pallas kernels  183 us (93%)
  other arithmetic  9.51 us (5%)
  local copies, waits for them, and re-layouts  2.2 us (1%)
    pallas_call x1, Pallas kernels, shards(): pl.pallas_call(functools.partial(kernel, n_grp, n_dev, owned, depth), out...  183 us

commit v1 on v0

v1 whole, which is shorter than its diff:
```python
import functools

import jax
import jax.numpy as jnp
from jax import lax
from jax.experimental import pallas as pl
from jax.experimental.pallas import tpu as pltpu
from jax.sharding import PartitionSpec as P

BS = 256
MSG = 128
MESH = pl.DeviceIdType.MESH
F32, BF16, I32 = jnp.float32, jnp.bfloat16, jnp.int32


def bits(n):
    return n.bit_length() - 1


def nt(a, b):
    return lax.dot_general(a, b, (((1,), (1,)), ((), ())), preferred_element_type=F32)


class Sizes:
    def __init__(self, n_grp, n_dev, npts, rows):
        self.g, self.dev = n_grp, n_dev
        self.nx = n_grp // 2
        ny = 1
        while 8 * ny * ny <= n_dev:
            ny *= 2
        self.ny, self.nz = ny, n_dev // ny
        self.team = n_grp * ny
        self.owned = rows // BS
        self.per = self.owned // n_grp
        self.n_blocks = self.owned * n_dev
        self.depth = 2 * npts // self.n_blocks
        self.steps = self.nz * self.per * self.depth // MSG
        self.zs = self.nz // self.steps
        self.nblk = self.zs * self.per
        self.line = self.nz == 4
        self.fins = 2 if self.line else self.nz - 1


def kernel(
    cf,
    block_row, final_row, points_hbm, cent_hbm,
    distances, fresh_out,
    points, tab, slot_row, slot_col, out, recv, tgt_out, tgt_in,
    part, own_sum, agg_in, fin_in, cnt, cagg_in, cfin_in,
    dist, ret, xs, xin,
    s_pts, r_pts, s_tgt, r_tgt, s_tab, r_tab, s_sum, r_agg, r_fin, s_cnt, r_cagg, r_cfin,
    s_ret, r_ret, s_x, r_x, in_sem,
):
    G, nx, ny, nz, TM = cf.g, cf.nx, cf.ny, cf.nz, cf.team
    per, depth, steps, zs, nblk = cf.per, cf.depth, cf.steps, cf.zs, cf.nblk
    g, d = lax.axis_index("grp"), lax.axis_index("dev")
    x, c = g // 2, g % 2
    z, y = d // ny, d % ny
    npts, width = points.shape
    share = width // G
    quarter = per * BS
    R = TM * MSG

    def to(gg, zz, yy):
        return {"grp": gg, "dev": zz * ny + yy}

    def split(o):
        return o // (2 * nx), o // 2 % nx, o % 2

    def mate(o):
        dy, dx, dc = split(o)
        return to((x + dx) % nx * 2 + (c + dc) % 2, z, (y + dy) % ny)

    def copy(src, dst, ss, rs, dev):
        return pltpu.make_async_remote_copy(
            src_ref=src, dst_ref=dst, send_sem=ss, recv_sem=rs, device_id=dev, device_id_type=MESH
        )

    half = z // (nz // 2)
    if cf.line:
        z_mate, z_inner, z_edge = half * 2 + 1 - z % 2, 2 - half, 3 * (1 - half)
        inner = (z + half) % 2 == 1
        edge = (z + half) % 2 == 0
        order = [z_edge, z_inner, z_mate, z]

    def zq(q):
        return order[q] if cf.line else (z + q + 1) % nz

    load_tab = pltpu.make_async_copy(
        cent_hbm.at[pl.ds(pl.multiple_of(g * quarter, quarter), quarter)], tab.at[z], in_sem.at[0]
    )
    load_points = pltpu.make_async_copy(points_hbm, points, in_sem.at[1])
    load_tab.start()
    load_points.start()

    barrier = pltpu.get_barrier_semaphore()
    peers = [mate(o) for o in range(1, TM)] + [to(g, (z + k) % nz, y) for k in range(1, nz)]
    for p in peers:
        pl.semaphore_signal(barrier, inc=1, device_id=p, device_id_type=MESH)
    pl.semaphore_wait(barrier, len(peers))

    def tabc(k, zt, zd, p):
        piece = tab.at[zt, pl.ds(p * BS, BS)]
        return copy(piece, piece, s_tab.at[k, p], r_tab.at[zt, p], to(g, zd, y))

    load_tab.wait()
    if cf.line:
        own_up = [tabc(0, z, z_mate, p) for p in range(per)]
        own_cross = [tabc(1, z, z_inner, p) for p in range(per)]
        f_mate = [tabc(2, z_mate, z_inner, p) for p in range(per)]
        f_inner = [tabc(3, z_inner, z_mate, p) for p in range(per)]
        f_edge = [tabc(4, z_edge, z_mate, p) for p in range(per)]
        for q in own_up:
            q.start()

        @pl.when(inner)
        def _():
            for q in own_cross:
                q.start()
    else:
        spread = [tabc(k, z, (z + k) % nz, p) for k in range(1, nz) for p in range(per)]
        for q in spread:
            q.start()

    def forward(kinds, p):
        if cf.line:

            @pl.when(inner)
            def _():
                for kind in kinds:
                    kind[p].wait_recv()
                    kind[p].start()

    b = block_row[...]
    hold, sub = b >> bits(cf.owned), b & (cf.owned - 1)
    zb, yb = hold >> bits(ny), hold & (ny - 1)
    gb, jb = sub >> bits(per), sub & (per - 1)
    ob = ((yb - y + ny) & (ny - 1)) * nx + (((gb >> 1) - x + nx) & (nx - 1))
    ob = ob * 2 + (((gb & 1) - c + 2) & 1)
    if cf.line:
        hb = zb >> 1
        qb = jnp.where(hb == half, jnp.where(zb == z, 3, 2), (zb + hb) & 1)
    else:
        qb = (zb - z - 1 + nz) & (nz - 1)
    place = ((qb >> bits(zs)) * TM + ob) * MSG + ((qb & (zs - 1)) * per + jb) * depth

    step = min(256, npts)
    before = (
        lax.broadcasted_iota(I32, (step, step), 0) < lax.broadcasted_iota(I32, (step, step), 1)
    ).astype(BF16)
    seen = jnp.zeros((cf.n_blocks, 1), F32)
    for t in range(npts // step):
        here = slice(t * step, (t + 1) * step)
        member = (lax.broadcasted_iota(I32, (cf.n_blocks, step), 0) == b[:, here]).astype(F32)
        prior = jnp.dot(member.astype(BF16), before, preferred_element_type=F32) + seen
        rank = jnp.sum(member * prior, axis=0, keepdims=True)
        seen = seen + jnp.sum(member, axis=1, keepdims=True)
        slot = place[:, here] + rank.astype(I32)
        slot_row[:, here] = slot
        slot_col[here, :] = jnp.transpose(jnp.broadcast_to(slot.astype(F32), (8, step)))
    want_row = jnp.broadcast_to((final_row[...] + 1).astype(F32), (8, npts)).astype(BF16)
    load_points.wait()

    pts_c = {
        (s, o): copy(out.at[s, o], recv.at[s, o], s_pts.at[s, o], r_pts.at[s, o], mate(o))
        for s in range(steps)
        for o in range(1, TM)
    }
    tgt_c = {
        (s, o): copy(tgt_out.at[s, o], tgt_in.at[s, o], s_tgt.at[s, o], r_tgt.at[s, o], mate(o))
        for s in range(steps)
        for o in range(1, TM)
    }
    ret_c = {
        (s, o): copy(
            dist.at[s, o],
            ret.at[s, o],
            s_ret.at[s, o],
            r_ret.at[s, o],
            to((x + nx - split(o)[1]) % nx * 2 + (c + split(o)[2]) % 2, z, (y + ny - split(o)[0]) % ny),
        )
        for s in range(steps)
        for o in range(1, TM)
    }

    def pack(s):
        for lo in list(range(TM - 2, -1, -2)):
            base = (s * TM + lo) * MSG
            hot = (lax.broadcasted_iota(I32, (2 * MSG, npts), 0) + base == slot_row[...]).astype(BF16)
            pts = jnp.dot(hot, points[...], preferred_element_type=F32).astype(BF16)
            tg = nt(want_row, hot)
            for i in range(2):
                o = lo + i
                rows, lanes = pts[i * MSG : (i + 1) * MSG], tg[:, i * MSG : (i + 1) * MSG]
                if o:
                    out[s, o] = rows
                    tgt_out[s, o] = lanes
                    tgt_c[s, o].start()
                    pts_c[s, o].start()
                else:
                    recv[s, 0] = rows
                    tgt_in[s, 0] = lanes

    def each(n, body):
        if n <= 2:
            for i in range(n):
                body(i)
        else:
            pl.loop(0, n)(body)

    ones = jnp.ones((8, R), BF16)

    def sums(s):
        for o in range(1, TM):
            tgt_c[s, o].wait_recv()
            pts_c[s, o].wait_recv()
        row = jnp.concatenate([tgt_in[s, o][0:1] for o in range(TM)], axis=1).astype(I32) - 1
        in_blk = (lax.broadcasted_iota(I32, (1, R), 1) & (MSG - 1)) >> bits(depth)

        def block(blk, own):
            want = jnp.where(in_blk == blk, row, -1)
            hot = (lax.broadcasted_iota(I32, (BS, R), 0) == want).astype(BF16)
            q, j = s * zs + blk // per, blk % per
            here = pl.ds(j * BS if isinstance(j, int) else pl.multiple_of(j * BS, BS), BS)
            cnt[q, j] = nt(ones, hot)
            total = jnp.dot(hot, recv[s].reshape(R, width), preferred_element_type=F32)
            if own:
                own_sum[here, :] = total
            else:
                part[q, here, :] = total.astype(BF16)

        n_own = per if s == steps - 1 else 0
        each(nblk - n_own, lambda blk: block(blk, False))
        for blk in range(nblk - n_own, nblk):
            block(blk, True)

    def dists(s):
        def block(blk):
            q, j = s * zs + blk // per, blk % per
            here = pl.ds(j * BS if isinstance(j, int) else pl.multiple_of(j * BS, BS), BS)
            rows = pl.ds(blk * depth if isinstance(blk, int) else pl.multiple_of(blk * depth, depth), depth)
            pts = recv[s, :, rows, :].reshape(TM * depth, width)
            table = tab[zq(q), here, :]
            cross = nt(pts, table)
            wide, twide = pts.astype(F32), table.astype(F32)
            rn = jnp.sum(wide * wide, axis=1, keepdims=True)
            cn = jnp.sum(twide * twide, axis=1, keepdims=True)
            cn = jnp.transpose(jnp.broadcast_to(cn, (BS, MSG)))[0:1]
            res = ((rn - 2.0 * cross + cn) / width).astype(BF16)
            dist[s, :, rows, :] = res.reshape(TM, depth, BS)

        each(nblk, block)
        for o in list(range(2, TM)) + [1]:
            ret_c[s, o].start()
        ret[s, 0] = dist[s, 0]

    gathered = []

    def gather(s):
        for o in range(1, TM):
            ret_c[s, o].wait_recv()
        first = not gathered
        gathered.append(s)
        ptile = min(256, npts)

        @pl.loop(0, npts // ptile)
        def _(t):
            here = pl.ds(pl.multiple_of(t * ptile, ptile), ptile)
            where = slot_col[here, 0:1].astype(I32)
            hot = (lax.broadcasted_iota(I32, (ptile, R), 1) + s * R == where).astype(BF16)
            acc = jnp.dot(hot, ret[s].reshape(R, BS), preferred_element_type=F32)
            if not first:
                acc += distances[here, :].astype(F32)
            distances[here, :] = acc.astype(BF16)

    if cf.line:
        to_agg = {
            q: [
                copy(part.at[q], agg_in.at[q], s_sum.at[q], r_agg.at[q], to(g, z_mate, y)),
                copy(cnt.at[q], cagg_in.at[q], s_cnt.at[q], r_cagg.at[q], to(g, z_mate, y)),
            ]
            for q in (0, 1)
        }
        to_far = {
            q: [
                copy(part.at[q], fin_in.at[1], s_sum.at[q], r_fin.at[1], to(g, order[q], y)),
                copy(cnt.at[q], cfin_in.at[1], s_cnt.at[q], r_cfin.at[1], to(g, order[q], y)),
            ]
            for q in (0, 1)
        }
        to_mate = [
            copy(part.at[2], fin_in.at[0], s_sum.at[2], r_fin.at[0], to(g, z_mate, y)),
            copy(cnt.at[2], cfin_in.at[0], s_cnt.at[2], r_cfin.at[0], to(g, z_mate, y)),
        ]
        finals = to_mate + to_far[0]

        def lift(q):
            @pl.when(edge)
            def _():
                for k in to_agg[q]:
                    k.start()

        def merge(q):
            @pl.when(inner)
            def _():
                for k in to_agg[q]:
                    k.wait_recv()

                @pl.loop(0, per)
                def _(j):
                    here = pl.ds(pl.multiple_of(j * BS, BS), BS)
                    both = part[q, here, :].astype(F32) + agg_in[q, here, :].astype(F32)
                    part[q, here, :] = both.astype(BF16)

                cnt[q] = cnt[q] + cagg_in[q]
                for k in to_far[q]:
                    k.start()

        def tables(q):
            @pl.when(edge)
            def _():
                for p in range(per):
                    tabc(3, order[q], z, p).wait_recv()

    else:
        direct = []
        for q in range(nz - 1):
            direct.append(copy(part.at[q], fin_in.at[q], s_sum.at[q], r_fin.at[q], to(g, zq(q), y)))
            direct.append(copy(cnt.at[q], cfin_in.at[q], s_cnt.at[q], r_cfin.at[q], to(g, zq(q), y)))
        finals = direct

    def group(k):
        dx, dc = k // 2, k % 2
        return (x + dx) % nx * 2 + (c + dc) % 2

    x_c = {k: copy(xs.at[group(k)], xin.at[k - 1], s_x.at[k], r_x.at[k], to(group(k), z, y)) for k in range(1, G)}

    def finish():
        for q in finals:
            q.wait_recv()
        for j in range(per):
            here = pl.ds(j * BS, BS)
            total, many = own_sum[here, :], cnt[nz - 1, j]
            for f in range(cf.fins):
                total += fin_in[f, here, :].astype(F32)
                many += cfin_in[f, j]
            many = 1.0 / (jnp.transpose(many)[:, 0:1] + 1.0)
            fresh = ((total + tab[z, here, :].astype(F32)) * many).astype(BF16)
            for k in range(G):
                xs[k, here, :] = fresh[:, k * share : (k + 1) * share]
        for k in list(range(2, G)) + [1]:
            x_c[k].start()

    def settle(gg, block):
        fresh_out[pl.ds(pl.multiple_of(gg * quarter, quarter), quarter), :] = block.astype(F32)

    if cf.line:
        pack(0)
        pack(1)
        pack(2)
        forward([f_mate, f_inner], 0)
        pack(3)
        for p in range(1, per):
            forward([f_mate, f_inner], p)
        sums(0)
        lift(0)
        for p in range(per):
            forward([f_edge], p)
        sums(1)
        lift(1)
        merge(0)
        tables(1)
        dists(1)
        sums(2)
        for k in to_mate:
            k.start()
        merge(1)
        tables(0)
        tables(2)
        dists(0)
        dists(2)
        sums(3)
        dists(3)
        finish()
        late = [1, 0, 2]
    else:
        for s in range(steps):
            pack(s)
        for s in range(steps):
            sums(s)
        for k in direct:
            k.start()
        for q in spread:
            q.wait_recv()
        for s in range(steps):
            dists(s)
        finish()
        late = list(range(steps - 1))
    for s in late:
        gather(s)
    settle(g, xs[g])
    for k in range(1, G):
        x_c[k].wait_recv()
        dx, dc = k // 2, k % 2
        settle((x + nx - dx) % nx * 2 + (c + dc) % 2, xin[k - 1])
    gather(steps - 1)

    for group_c in (pts_c, tgt_c, ret_c, x_c):
        for q in group_c.values():
            q.wait_send()
    if cf.line:
        for q in own_up + to_mate:
            q.wait_send()

        @pl.when(inner)
        def _():
            for q in own_cross + f_mate + f_inner + f_edge + to_far[0] + to_far[1]:
                q.wait_send()

        @pl.when(edge)
        def _():
            for q in to_agg[0] + to_agg[1]:
                q.wait_send()
    else:
        for q in spread + direct:
            q.wait_send()


def shards(points, blocks, finals, centroids):
    n_dev = lax.axis_size("dev")
    n_grp = lax.axis_size("grp")
    npts, width = points.shape
    rows = centroids.shape[0]
    cf = Sizes(n_grp, n_dev, npts, rows)
    share = width // n_grp
    quarter = cf.per * BS
    nz, tm, steps = cf.nz, cf.team, cf.steps

    dma = pltpu.SemaphoreType.DMA
    vm = pltpu.VMEM
    return pl.pallas_call(
        functools.partial(kernel, cf),
        out_shape=(
            jax.ShapeDtypeStruct((npts, BS), BF16),
            jax.ShapeDtypeStruct((rows, share), F32),
        ),
        in_specs=[pl.BlockSpec(memory_space=vm)] * 2 + [pl.BlockSpec(memory_space=pl.ANY)] * 2,
        out_specs=(pl.BlockSpec(memory_space=vm),) * 2,
        scratch_shapes=[
            vm((npts, width), BF16),
            vm((nz, quarter, width), BF16),
            vm((1, npts), I32),
            vm((npts, 8), F32),
            vm((steps, tm, MSG, width), BF16),
            vm((steps, tm, MSG, width), BF16),
            vm((steps, tm, 8, MSG), F32),
            vm((steps, tm, 8, MSG), F32),
            vm((nz - 1, quarter, width), BF16),
            vm((quarter, width), F32),
            vm((2, quarter, width), BF16),
            vm((cf.fins, quarter, width), BF16),
            vm((nz, cf.per, 8, BS), F32),
            vm((2, cf.per, 8, BS), F32),
            vm((cf.fins, cf.per, 8, BS), F32),
            vm((steps, tm, MSG, BS), BF16),
            vm((steps, tm, MSG, BS), BF16),
            vm((n_grp, quarter, share), BF16),
            vm((n_grp - 1, quarter, share), BF16),
            dma((steps, tm)), dma((steps, tm)), dma((steps, tm)), dma((steps, tm)),
            dma((max(5, nz), cf.per)), dma((nz, cf.per)),
            dma((nz - 1,)), dma((2,)), dma((cf.fins,)), dma((nz - 1,)), dma((2,)), dma((cf.fins,)),
            dma((steps, tm)), dma((steps, tm)), dma((n_grp,)), dma((n_grp,)), dma((2,)),
        ],
        compiler_params=pltpu.CompilerParams(
            collective_id=0, has_side_effects=True, vmem_limit_bytes=67_000_000
        ),
    )(blocks.reshape(1, npts), finals.reshape(1, npts), points, centroids)


def solution(mesh):
    placed = (P(("grp", "dev"), None), P(("grp", "dev"), None), P(("grp", "dev")), P("dev", None))
    return jax.shard_map(
        shards,
        mesh=mesh,
        in_specs=placed,
        out_specs=(P(("grp", "dev"), None), P("dev", "grp")),
        check_vma=False,
    )
```

time: 196 us -> 148 us (0.76)
  Pallas kernels: 183 us -> 141 us
  other arithmetic: 9.51 us -> 0 us
  local copies, waits for them, and re-layouts: 2.2 us -> 5.31 us
    pallas_call x1, Pallas kernels: 183 us -> 141 us  [shards(): pl.pallas_call(functools.partial(kernel, cf), out_shape=(jax.ShapeDtypeSt...]
    unnamed x4 -> x2, local copies, waits for them, and re-layouts: 0.98 us -> 5.31 us
    div x1 -> x0, other arithmetic: 3.61 us -> none  [shards(): (col_sums + own_cols) / (counts.reshape(rows) + 1.0)[:, None]]
    reduce_sum x1 -> x0, other arithmetic: 3.07 us -> none  [shards(): cn = jnp.sum(jnp.square(centroids.astype(F32)), axis=-1).reshape(owned, BS)]
where the time goes in v1:
time: 148 us; the launch traced here: 147 us
  Pallas kernels  141 us (95%)
  local copies, waits for them, and re-layouts  5.31 us (4%)
    pallas_call x1, Pallas kernels, shards(): pl.pallas_call(functools.partial(kernel, cf), out_shape=(jax.ShapeDtypeSt...  141 us
    unnamed x2, local copies, waits for them, and re-layouts  5.31 us

profile of v1, /device:TPU:0, one launch (start us, length us, event | category | flops | bytes accessed | tf_op | source)
XLA Modules:
  0.0 146.9 jit_solution(5703906780134595661)
XLA Ops:
  0.6 140.9 %shard_map.59 = (bf16[2048,256]{1,0:T(8,128)(2,1)}, f32[2048,256]{1,0:T(8,128)}) custom-call(s32[1,2048]{1,0:T(1,128)} %bitcast.2, s32[1,2048]{1,0:T(1,128)} %bitcast.3, bf16[2048,1024]{1,0:T(8,128)(2,1)} %points_hbm.1, bf16[2048,1024]{1,0:T(8,128)(2,1)} %cent_hbm.1), custom_call_target="tpu_custom_call" | custom-call | tf_op jit(solution)/shard_map/pallas_call | solution.py:441
  141.5 2.3 %copy.8 = bf16[2048,256]{1,0:T(8,128)(2,1)} copy(bf16[2048,256]{1,0:T(8,128)(2,1)} %get-tuple-element.4) | data formatting | bytes 2097152
  143.8 3.0 %copy.9 = f32[2048,256]{1,0:T(8,128)} copy(f32[2048,256]{1,0:T(8,128)} %get-tuple-element.5) | data formatting | bytes 4194304

commit v2 on v1

--- a/solution.py
+++ b/solution.py
@@ -97,30 +97,10 @@
     peers = [mate(o) for o in range(1, TM)] + [to(g, (z + k) % nz, y) for k in range(1, nz)]
     for p in peers:
         pl.semaphore_signal(barrier, inc=1, device_id=p, device_id_type=MESH)
-    pl.semaphore_wait(barrier, len(peers))
 
     def tabc(k, zt, zd, p):
         piece = tab.at[zt, pl.ds(p * BS, BS)]
         return copy(piece, piece, s_tab.at[k, p], r_tab.at[zt, p], to(g, zd, y))
-
-    load_tab.wait()
-    if cf.line:
-        own_up = [tabc(0, z, z_mate, p) for p in range(per)]
-        own_cross = [tabc(1, z, z_inner, p) for p in range(per)]
-        f_mate = [tabc(2, z_mate, z_inner, p) for p in range(per)]
-        f_inner = [tabc(3, z_inner, z_mate, p) for p in range(per)]
-        f_edge = [tabc(4, z_edge, z_mate, p) for p in range(per)]
-        for q in own_up:
-            q.start()
-
-        @pl.when(inner)
-        def _():
-            for q in own_cross:
-                q.start()
-    else:
-        spread = [tabc(k, z, (z + k) % nz, p) for k in range(1, nz) for p in range(per)]
-        for q in spread:
-            q.start()
 
     def forward(kinds, p):
         if cf.line:
@@ -183,23 +163,55 @@
         for o in range(1, TM)
     }
 
+    def tile(s, lo):
+        base = (s * TM + lo) * MSG
+        hot = (lax.broadcasted_iota(I32, (2 * MSG, npts), 0) + base == slot_row[...]).astype(BF16)
+        pts = jnp.dot(hot, points[...], preferred_element_type=F32).astype(BF16)
+        tg = nt(want_row, hot)
+        for i in range(2):
+            o = lo + i
+            rows, lanes = pts[i * MSG : (i + 1) * MSG], tg[:, i * MSG : (i + 1) * MSG]
+            if o:
+                out[s, o] = rows
+                tgt_out[s, o] = lanes
+            else:
+                recv[s, 0] = rows
+                tgt_in[s, 0] = lanes
+
+    def send(s, lo):
+        for o in (lo, lo + 1):
+            if o:
+                tgt_c[s, o].start()
+                pts_c[s, o].start()
+
     def pack(s):
-        for lo in list(range(TM - 2, -1, -2)):
-            base = (s * TM + lo) * MSG
-            hot = (lax.broadcasted_iota(I32, (2 * MSG, npts), 0) + base == slot_row[...]).astype(BF16)
-            pts = jnp.dot(hot, points[...], preferred_element_type=F32).astype(BF16)
-            tg = nt(want_row, hot)
-            for i in range(2):
-                o = lo + i
-                rows, lanes = pts[i * MSG : (i + 1) * MSG], tg[:, i * MSG : (i + 1) * MSG]
-                if o:
-                    out[s, o] = rows
-                    tgt_out[s, o] = lanes
-                    tgt_c[s, o].start()
-                    pts_c[s, o].start()
-                else:
-                    recv[s, 0] = rows
-                    tgt_in[s, 0] = lanes
+        for lo in range(TM - 2, -1, -2):
+            if (s, lo) != (0, TM - 2):
+                tile(s, lo)
+                send(s, lo)
+
+    tile(0, TM - 2)
+    pl.semaphore_wait(barrier, len(peers))
+    send(0, TM - 2)
+
+    load_tab.wait()
+    if cf.line:
+        own_up = [tabc(0, z, z_mate, p) for p in range(per)]
+        own_cross = [tabc(1, z, z_inner, p) for p in range(per)]
+        f_mate = [tabc(2, z_mate, z_inner, p) for p in range(per)]
+        f_inner = [tabc(3, z_inner, z_mate, p) for p in range(per)]
+        f_edge = [tabc(4, z_edge, z_mate, p) for p in range(per)]
+        for q in own_up:
+            q.start()
+
+        @pl.when(inner)
+        def _():
+            for q in own_cross:
+                q.start()
+    else:
+        spread = [tabc(k, z, (z + k) % nz, p) for k in range(1, nz) for p in range(per)]
+        for q in spread:
+            q.start()
 
     def each(n, body):
         if n <= 2:
@@ -274,36 +286,33 @@
             distances[here, :] = acc.astype(BF16)
 
     if cf.line:
-        to_agg = {
-            q: [
-                copy(part.at[q], agg_in.at[q], s_sum.at[q], r_agg.at[q], to(g, z_mate, y)),
-                copy(cnt.at[q], cagg_in.at[q], s_cnt.at[q], r_cagg.at[q], to(g, z_mate, y)),
+
+        def pair(q, dst, cdst, rs, crs, zd):
+            return [
+                copy(part.at[q], dst, s_sum.at[q], rs, to(g, zd, y)),
+                copy(cnt.at[q], cdst, s_cnt.at[q], crs, to(g, zd, y)),
             ]
-            for q in (0, 1)
-        }
-        to_far = {
-            q: [
-                copy(part.at[q], fin_in.at[1], s_sum.at[q], r_fin.at[1], to(g, order[q], y)),
-                copy(cnt.at[q], cfin_in.at[1], s_cnt.at[q], r_cfin.at[1], to(g, order[q], y)),
-            ]
-            for q in (0, 1)
-        }
-        to_mate = [
-            copy(part.at[2], fin_in.at[0], s_sum.at[2], r_fin.at[0], to(g, z_mate, y)),
-            copy(cnt.at[2], cfin_in.at[0], s_cnt.at[2], r_cfin.at[0], to(g, z_mate, y)),
-        ]
-        finals = to_mate + to_far[0]
+
+        def agg(q, k, zd):
+            return pair(q, agg_in.at[k], cagg_in.at[k], r_agg.at[k], r_cagg.at[k], zd)
+
+        def fin(q, k, zd):
+            return pair(q, fin_in.at[k], cfin_in.at[k], r_fin.at[k], r_cfin.at[k], zd)
+
+        edge_out = [agg(0, 0, z_mate), agg(1, 1, z_mate), fin(2, 0, z_mate)]
+        inner_out = [agg(0, 2, z_inner), fin(1, 1, z_inner), fin(2, 0, z_mate)]
+        inner_in = [agg(0, 0, z_mate), agg(1, 1, z_mate), agg(2, 2, z_inner)]
 
         def lift(q):
             @pl.when(edge)
             def _():
-                for k in to_agg[q]:
+                for k in edge_out[q]:
                     k.start()
 
         def merge(q):
             @pl.when(inner)
             def _():
-                for k in to_agg[q]:
+                for k in inner_in[q]:
                     k.wait_recv()
 
                 @pl.loop(0, per)
@@ -313,7 +322,7 @@
                     part[q, here, :] = both.astype(BF16)
 
                 cnt[q] = cnt[q] + cagg_in[q]
-                for k in to_far[q]:
+                for k in inner_out[q]:
                     k.start()
 
         def tables(q):
@@ -322,12 +331,31 @@
                 for p in range(per):
                     tabc(3, order[q], z, p).wait_recv()
 
+        def arrive():
+            for k in edge_out[2]:
+                k.wait_recv()
+
+            @pl.when(inner)
+            def _():
+                for k in inner_out[1]:
+                    k.wait_recv()
+
+                @pl.loop(0, per)
+                def _(j):
+                    here = pl.ds(pl.multiple_of(j * BS, BS), BS)
+                    own_sum[here, :] += fin_in[1, here, :].astype(F32)
+
+                cnt[nz - 1] = cnt[nz - 1] + cfin_in[1]
+
     else:
         direct = []
         for q in range(nz - 1):
             direct.append(copy(part.at[q], fin_in.at[q], s_sum.at[q], r_fin.at[q], to(g, zq(q), y)))
             direct.append(copy(cnt.at[q], cfin_in.at[q], s_cnt.at[q], r_cfin.at[q], to(g, zq(q), y)))
-        finals = direct
+
+        def arrive():
+            for q in direct:
+                q.wait_recv()
 
     def group(k):
         dx, dc = k // 2, k % 2
@@ -336,12 +364,11 @@
     x_c = {k: copy(xs.at[group(k)], xin.at[k - 1], s_x.at[k], r_x.at[k], to(group(k), z, y)) for k in range(1, G)}
 
     def finish():
-        for q in finals:
-            q.wait_recv()
+        arrive()
         for j in range(per):
             here = pl.ds(j * BS, BS)
             total, many = own_sum[here, :], cnt[nz - 1, j]
-            for f in range(cf.fins):
+            for f in range(1 if cf.line else cf.fins):
                 total += fin_in[f, here, :].astype(F32)
                 many += cfin_in[f, j]
             many = 1.0 / (jnp.transpose(many)[:, 0:1] + 1.0)
@@ -372,9 +399,9 @@
         tables(1)
         dists(1)
         sums(2)
-        for k in to_mate:
-            k.start()
+        lift(2)
         merge(1)
+        merge(2)
         tables(0)
         tables(2)
         dists(0)
@@ -396,30 +423,24 @@
             dists(s)
         finish()
         late = list(range(steps - 1))
-    for s in late:
+    for s in late + [steps - 1]:
         gather(s)
     settle(g, xs[g])
     for k in range(1, G):
         x_c[k].wait_recv()
         dx, dc = k // 2, k % 2
         settle((x + nx - dx) % nx * 2 + (c + dc) % 2, xin[k - 1])
-    gather(steps - 1)
 
     for group_c in (pts_c, tgt_c, ret_c, x_c):
         for q in group_c.values():
             q.wait_send()
     if cf.line:
-        for q in own_up + to_mate:
+        for q in own_up + edge_out[0] + edge_out[1] + edge_out[2]:
             q.wait_send()
 
         @pl.when(inner)
         def _():
-            for q in own_cross + f_mate + f_inner + f_edge + to_far[0] + to_far[1]:
-                q.wait_send()
-
-        @pl.when(edge)
-        def _():
-            for q in to_agg[0] + to_agg[1]:
+            for q in own_cross + f_mate + f_inner + f_edge:
                 q.wait_send()
     else:
         for q in spread + direct:
@@ -440,10 +461,7 @@
     vm = pltpu.VMEM
     return pl.pallas_call(
         functools.partial(kernel, cf),
-        out_shape=(
-            jax.ShapeDtypeStruct((npts, BS), BF16),
-            jax.ShapeDtypeStruct((rows, share), F32),
-        ),
+        out_shape=(vm((npts, BS), BF16), vm((rows, share), F32)),
         in_specs=[pl.BlockSpec(memory_space=vm)] * 2 + [pl.BlockSpec(memory_space=pl.ANY)] * 2,
         out_specs=(pl.BlockSpec(memory_space=vm),) * 2,
         scratch_shapes=[
@@ -457,10 +475,10 @@
             vm((steps, tm, 8, MSG), F32),
             vm((nz - 1, quarter, width), BF16),
             vm((quarter, width), F32),
-            vm((2, quarter, width), BF16),
+            vm((3, quarter, width), BF16),
             vm((cf.fins, quarter, width), BF16),
             vm((nz, cf.per, 8, BS), F32),
-            vm((2, cf.per, 8, BS), F32),
+            vm((3, cf.per, 8, BS), F32),
             vm((cf.fins, cf.per, 8, BS), F32),
             vm((steps, tm, MSG, BS), BF16),
             vm((steps, tm, MSG, BS), BF16),
@@ -468,11 +486,11 @@
             vm((n_grp - 1, quarter, share), BF16),
             dma((steps, tm)), dma((steps, tm)), dma((steps, tm)), dma((steps, tm)),
             dma((max(5, nz), cf.per)), dma((nz, cf.per)),
-            dma((nz - 1,)), dma((2,)), dma((cf.fins,)), dma((nz - 1,)), dma((2,)), dma((cf.fins,)),
+            dma((nz - 1,)), dma((3,)), dma((cf.fins,)), dma((nz - 1,)), dma((3,)), dma((cf.fins,)),
             dma((steps, tm)), dma((steps, tm)), dma((n_grp,)), dma((n_grp,)), dma((2,)),
         ],
         compiler_params=pltpu.CompilerParams(
-            collective_id=0, has_side_effects=True, vmem_limit_bytes=67_000_000
+            collective_id=0, has_side_effects=True, vmem_limit_bytes=58_000_000
         ),
     )(blocks.reshape(1, npts), finals.reshape(1, npts), points, centroids)
 

time: 148 us -> 139 us (0.939)
  Pallas kernels: 141 us -> 135 us
  local copies, waits for them, and re-layouts: 5.31 us -> 2.29 us
    pallas_call x1, Pallas kernels: 141 us -> 135 us  [shards(): pl.pallas_call(functools.partial(kernel, cf), out_shape=(vm((npts, BS), B...]
    unnamed x2, local copies, waits for them, and re-layouts: 5.31 us -> 2.29 us
where the time goes in v2:
time: 139 us; the launch traced here: 138 us
  Pallas kernels  135 us (97%)
  local copies, waits for them, and re-layouts  2.29 us (2%)
    pallas_call x1, Pallas kernels, shards(): pl.pallas_call(functools.partial(kernel, cf), out_shape=(vm((npts, BS), B...  135 us

profile of v2, /device:TPU:0, one launch (start us, length us, event | category | flops | bytes accessed | tf_op | source)
XLA Modules:
  0.0 138.3 jit_solution(3731583866650275136)
XLA Ops:
  0.6 135.4 %shard_map.59 = (bf16[2048,256]{1,0:T(8,128)(2,1)S(1)}, f32[2048,256]{1,0:T(8,128)S(1)}) custom-call(s32[1,2048]{1,0:T(1,128)} %bitcast.2, s32[1,2048]{1,0:T(1,128)} %bitcast.3, bf16[2048,1024]{1,0:T(8,128)(2,1)} %points_hbm.1, bf16[2048,1024]{1,0:T(8,128)(2,1)} %cent_hbm.1), custom_call_target="tpu_custom_call" | custom-call | tf_op jit(solution)/shard_map/pallas_call | solution.py:462
  136.0 1.0 copy.8
  137.0 1.3 copy.9

commit v3 on v2

--- a/solution.py
+++ b/solution.py
@@ -37,7 +37,7 @@
         self.steps = self.nz * self.per * self.depth // MSG
         self.zs = self.nz // self.steps
         self.nblk = self.zs * self.per
-        self.line = self.nz == 4
+        self.line = self.nz == 4 and self.nx == 2
         self.fins = 2 if self.line else self.nz - 1
 
 
@@ -47,9 +47,9 @@
     distances, fresh_out,
     points, tab, slot_row, slot_col, out, recv, tgt_out, tgt_in,
     part, own_sum, agg_in, fin_in, cnt, cagg_in, cfin_in,
-    dist, ret, xs, xin,
+    dist, ret, xs, xin, tab_x, oth_sum, cnt_oth, x_out, x_in, cx_in,
     s_pts, r_pts, s_tgt, r_tgt, s_tab, r_tab, s_sum, r_agg, r_fin, s_cnt, r_cagg, r_cfin,
-    s_ret, r_ret, s_x, r_x, in_sem,
+    s_ret, r_ret, s_x, r_x, s_side, r_side, s_cside, r_cside, in_sem,
 ):
     G, nx, ny, nz, TM = cf.g, cf.nx, cf.ny, cf.nz, cf.team
     per, depth, steps, zs, nblk = cf.per, cf.depth, cf.steps, cf.zs, cf.nblk
@@ -67,9 +67,22 @@
     def split(o):
         return o // (2 * nx), o // 2 % nx, o % 2
 
-    def mate(o):
+    def near(s):
+        return cf.line and s == steps - 1
+
+    def mate(o, s=0):
         dy, dx, dc = split(o)
-        return to((x + dx) % nx * 2 + (c + dc) % 2, z, (y + dy) % ny)
+        return to((x + (0 if near(s) else dx)) % nx * 2 + (c + dc) % 2, z, (y + dy) % ny)
+
+    def back(o, s):
+        dy, dx, dc = split(o)
+        return to((x + nx - (0 if near(s) else dx)) % nx * 2 + (c + dc) % 2, z, (y + ny - dy) % ny)
+
+    def remote(s):
+        return [o for o in range(TM) if (split(o)[0] or split(o)[2] if near(s) else o)]
+
+    def start_of(xq, cq):
+        return pl.multiple_of((cq * nx + xq) * quarter, quarter)
 
     def copy(src, dst, ss, rs, dev):
         return pltpu.make_async_remote_copy(
@@ -79,19 +92,25 @@
     half = z // (nz // 2)
     if cf.line:
         z_mate, z_inner, z_edge = half * 2 + 1 - z % 2, 2 - half, 3 * (1 - half)
-        inner = (z + half) % 2 == 1
-        edge = (z + half) % 2 == 0
-        order = [z_edge, z_inner, z_mate, z]
+        mid = (z + half) % 2
+        inner = mid == 1
+        edge = mid == 0
+        order = [z_edge, mid * z_mate + (1 - mid) * z_inner, mid * z_inner + (1 - mid) * z_mate, z]
 
     def zq(q):
         return order[q] if cf.line else (z + q + 1) % nz
 
     load_tab = pltpu.make_async_copy(
-        cent_hbm.at[pl.ds(pl.multiple_of(g * quarter, quarter), quarter)], tab.at[z], in_sem.at[0]
+        cent_hbm.at[pl.ds(start_of(x, c), quarter)], tab.at[z], in_sem.at[0]
     )
     load_points = pltpu.make_async_copy(points_hbm, points, in_sem.at[1])
+    load_points.start()
     load_tab.start()
-    load_points.start()
+    if cf.line:
+        load_other = pltpu.make_async_copy(
+            cent_hbm.at[pl.ds(start_of(1 - x, c), quarter)], tab_x, in_sem.at[2]
+        )
+        load_other.start()
 
     barrier = pltpu.get_barrier_semaphore()
     peers = [mate(o) for o in range(1, TM)] + [to(g, (z + k) % nz, y) for k in range(1, nz)]
@@ -115,11 +134,11 @@
     hold, sub = b >> bits(cf.owned), b & (cf.owned - 1)
     zb, yb = hold >> bits(ny), hold & (ny - 1)
     gb, jb = sub >> bits(per), sub & (per - 1)
-    ob = ((yb - y + ny) & (ny - 1)) * nx + (((gb >> 1) - x + nx) & (nx - 1))
-    ob = ob * 2 + (((gb & 1) - c + 2) & 1)
+    ob = ((yb - y + ny) & (ny - 1)) * nx + (((gb & (nx - 1)) - x + nx) & (nx - 1))
+    ob = ob * 2 + (((gb >> bits(nx)) - c + 2) & 1)
     if cf.line:
         hb = zb >> 1
-        qb = jnp.where(hb == half, jnp.where(zb == z, 3, 2), (zb + hb) & 1)
+        qb = jnp.where(hb == half, jnp.where(zb == z, 3, 2 - mid), ((zb + hb) & 1) * (1 + mid))
     else:
         qb = (zb - z - 1 + nz) & (nz - 1)
     place = ((qb >> bits(zs)) * TM + ob) * MSG + ((qb & (zs - 1)) * per + jb) * depth
@@ -141,27 +160,12 @@
     want_row = jnp.broadcast_to((final_row[...] + 1).astype(F32), (8, npts)).astype(BF16)
     load_points.wait()
 
-    pts_c = {
-        (s, o): copy(out.at[s, o], recv.at[s, o], s_pts.at[s, o], r_pts.at[s, o], mate(o))
-        for s in range(steps)
-        for o in range(1, TM)
-    }
-    tgt_c = {
-        (s, o): copy(tgt_out.at[s, o], tgt_in.at[s, o], s_tgt.at[s, o], r_tgt.at[s, o], mate(o))
-        for s in range(steps)
-        for o in range(1, TM)
-    }
-    ret_c = {
-        (s, o): copy(
-            dist.at[s, o],
-            ret.at[s, o],
-            s_ret.at[s, o],
-            r_ret.at[s, o],
-            to((x + nx - split(o)[1]) % nx * 2 + (c + split(o)[2]) % 2, z, (y + ny - split(o)[0]) % ny),
-        )
-        for s in range(steps)
-        for o in range(1, TM)
-    }
+    pts_c, tgt_c, ret_c = {}, {}, {}
+    for s in range(steps):
+        for o in remote(s):
+            pts_c[s, o] = copy(out.at[s, o], recv.at[s, o], s_pts.at[s, o], r_pts.at[s, o], mate(o, s))
+            tgt_c[s, o] = copy(tgt_out.at[s, o], tgt_in.at[s, o], s_tgt.at[s, o], r_tgt.at[s, o], mate(o, s))
+            ret_c[s, o] = copy(dist.at[s, o], ret.at[s, o], s_ret.at[s, o], r_ret.at[s, o], back(o, s))
 
     def tile(s, lo):
         base = (s * TM + lo) * MSG
@@ -171,16 +175,16 @@
         for i in range(2):
             o = lo + i
             rows, lanes = pts[i * MSG : (i + 1) * MSG], tg[:, i * MSG : (i + 1) * MSG]
-            if o:
+            if o in remote(s):
                 out[s, o] = rows
                 tgt_out[s, o] = lanes
             else:
-                recv[s, 0] = rows
-                tgt_in[s, 0] = lanes
+                recv[s, o] = rows
+                tgt_in[s, o] = lanes
 
     def send(s, lo):
         for o in (lo, lo + 1):
-            if o:
+            if o in remote(s):
                 tgt_c[s, o].start()
                 pts_c[s, o].start()
 
@@ -246,83 +250,129 @@
         for blk in range(nblk - n_own, nblk):
             block(blk, True)
 
+    def distance(pts, table):
+        cross = nt(pts, table)
+        wide, twide = pts.astype(F32), table.astype(F32)
+        rn = jnp.sum(wide * wide, axis=1, keepdims=True)
+        cn = jnp.sum(twide * twide, axis=1, keepdims=True)
+        cn = jnp.transpose(jnp.broadcast_to(cn, (BS, MSG)))[0:1]
+        return ((rn - 2.0 * cross + cn) / width).astype(BF16)
+
+    def give(s, units):
+        far = remote(s)
+        for o in [o for o in units if o in far]:
+            ret_c[s, o].start()
+        for o in units:
+            if o not in far:
+                ret[s, o] = dist[s, o]
+
     def dists(s):
         def block(blk):
             q, j = s * zs + blk // per, blk % per
             here = pl.ds(j * BS if isinstance(j, int) else pl.multiple_of(j * BS, BS), BS)
             rows = pl.ds(blk * depth if isinstance(blk, int) else pl.multiple_of(blk * depth, depth), depth)
             pts = recv[s, :, rows, :].reshape(TM * depth, width)
-            table = tab[zq(q), here, :]
-            cross = nt(pts, table)
-            wide, twide = pts.astype(F32), table.astype(F32)
-            rn = jnp.sum(wide * wide, axis=1, keepdims=True)
-            cn = jnp.sum(twide * twide, axis=1, keepdims=True)
-            cn = jnp.transpose(jnp.broadcast_to(cn, (BS, MSG)))[0:1]
-            res = ((rn - 2.0 * cross + cn) / width).astype(BF16)
-            dist[s, :, rows, :] = res.reshape(TM, depth, BS)
+            dist[s, :, rows, :] = distance(pts, tab[zq(q), here, :]).reshape(TM, depth, BS)
 
         each(nblk, block)
-        for o in list(range(2, TM)) + [1]:
-            ret_c[s, o].start()
-        ret[s, 0] = dist[s, 0]
+        give(s, list(range(2, TM)) + [0, 1])
+
+    def both(ref, s, dx, *rest):
+        return jnp.concatenate([ref[(s, slice(u, u + 2)) + rest] for u in range(dx * 2, TM, 2 * nx)], axis=0)
+
+    def near_sums(s, dx):
+        units = [u + dc for u in range(dx * 2, TM, 2 * nx) for dc in range(2)]
+        for o in units:
+            if o in remote(s):
+                tgt_c[s, o].wait_recv()
+                pts_c[s, o].wait_recv()
+        n = len(units) * MSG
+        row = jnp.concatenate([tgt_in[s, o][0:1] for o in units], axis=1).astype(I32) - 1
+        in_blk = (lax.broadcasted_iota(I32, (1, n), 1) & (MSG - 1)) >> bits(depth)
+        for j in range(per):
+            want = jnp.where(in_blk == j, row, -1)
+            hot = (lax.broadcasted_iota(I32, (BS, n), 0) == want).astype(BF16)
+            many = nt(jnp.ones((8, n), BF16), hot)
+            total = jnp.dot(hot, both(recv, s, dx).reshape(n, width), preferred_element_type=F32)
+            if dx:
+                cnt_oth[j] = many
+                oth_sum[j * BS : (j + 1) * BS, :] = total
+            else:
+                cnt[nz - 1, j] = many
+                own_sum[j * BS : (j + 1) * BS, :] = total
+
+    def near_dists(s, dx):
+        for j in range(per):
+            here, rows = slice(j * BS, (j + 1) * BS), slice(j * depth, (j + 1) * depth)
+            pts = both(recv, s, dx, rows).reshape(-1, width)
+            table = tab_x[here, :] if dx else tab[z, here, :]
+            res = distance(pts, table).reshape(-1, depth, BS)
+            for i, u in enumerate(range(dx * 2, TM, 2 * nx)):
+                dist[s, u : u + 2, rows, :] = res[2 * i : 2 * i + 2]
+        give(s, [u + dc for u in range(dx * 2, TM, 2 * nx) for dc in range(2)])
 
     gathered = []
 
-    def gather(s):
-        for o in range(1, TM):
-            ret_c[s, o].wait_recv()
+    def gather(s, lo, hi):
+        for o in remote(s):
+            if lo <= o < hi:
+                ret_c[s, o].wait_recv()
         first = not gathered
         gathered.append(s)
         ptile = min(256, npts)
-
-        @pl.loop(0, npts // ptile)
+        n = (hi - lo) * MSG
+
+        @pl.loop(0, npts // ptile, unroll=2)
         def _(t):
             here = pl.ds(pl.multiple_of(t * ptile, ptile), ptile)
             where = slot_col[here, 0:1].astype(I32)
-            hot = (lax.broadcasted_iota(I32, (ptile, R), 1) + s * R == where).astype(BF16)
-            acc = jnp.dot(hot, ret[s].reshape(R, BS), preferred_element_type=F32)
+            hot = (lax.broadcasted_iota(I32, (ptile, n), 1) + s * R + lo * MSG == where).astype(BF16)
+            acc = jnp.dot(hot, ret[s, lo:hi].reshape(n, BS), preferred_element_type=F32)
             if not first:
                 acc += distances[here, :].astype(F32)
             distances[here, :] = acc.astype(BF16)
 
     if cf.line:
 
-        def pair(q, dst, cdst, rs, crs, zd):
+        def pair(q, j, dst, cdst, rs, crs, zd):
+            piece = pl.ds(j * BS, BS)
             return [
-                copy(part.at[q], dst, s_sum.at[q], rs, to(g, zd, y)),
-                copy(cnt.at[q], cdst, s_cnt.at[q], crs, to(g, zd, y)),
+                copy(part.at[q, piece], dst.at[piece], s_sum.at[q, j], rs.at[j], to(g, zd, y)),
+                copy(cnt.at[q, j], cdst.at[j], s_cnt.at[q, j], crs.at[j], to(g, zd, y)),
             ]
 
-        def agg(q, k, zd):
-            return pair(q, agg_in.at[k], cagg_in.at[k], r_agg.at[k], r_cagg.at[k], zd)
-
-        def fin(q, k, zd):
-            return pair(q, fin_in.at[k], cfin_in.at[k], r_fin.at[k], r_cfin.at[k], zd)
-
-        edge_out = [agg(0, 0, z_mate), agg(1, 1, z_mate), fin(2, 0, z_mate)]
-        inner_out = [agg(0, 2, z_inner), fin(1, 1, z_inner), fin(2, 0, z_mate)]
-        inner_in = [agg(0, 0, z_mate), agg(1, 1, z_mate), agg(2, 2, z_inner)]
+        def agg(q, j, k, zd):
+            return pair(q, j, agg_in.at[k], cagg_in.at[k], r_agg.at[k], r_cagg.at[k], zd)
+
+        def fin(q, j, k, zd):
+            return pair(q, j, fin_in.at[k], cfin_in.at[k], r_fin.at[k], r_cfin.at[k], zd)
+
+        edge_out, inner_out, inner_in = {}, {}, {}
+        for j in range(per):
+            edge_out[0, j], edge_out[1, j], edge_out[2, j] = agg(0, j, 0, z_mate), agg(1, j, 1, z_mate), fin(2, j, 0, z_mate)
+            inner_out[0, j], inner_out[1, j], inner_out[2, j] = (
+                agg(0, j, 2, z_inner), fin(1, j, 0, z_mate), fin(2, j, 1, z_inner)
+            )
+            inner_in[0, j], inner_in[1, j], inner_in[2, j] = agg(0, j, 0, z_mate), agg(1, j, 2, z_inner), agg(2, j, 1, z_mate)
+        slot_of = [0, 2, 1]
 
         def lift(q):
             @pl.when(edge)
             def _():
-                for k in edge_out[q]:
-                    k.start()
-
-        def merge(q):
+                for j in range(per):
+                    for k in edge_out[q, j]:
+                        k.start()
+
+        def merge(q, j):
             @pl.when(inner)
             def _():
-                for k in inner_in[q]:
+                for k in inner_in[q, j]:
                     k.wait_recv()
-
-                @pl.loop(0, per)
-                def _(j):
-                    here = pl.ds(pl.multiple_of(j * BS, BS), BS)
-                    both = part[q, here, :].astype(F32) + agg_in[q, here, :].astype(F32)
-                    part[q, here, :] = both.astype(BF16)
-
-                cnt[q] = cnt[q] + cagg_in[q]
-                for k in inner_out[q]:
+                here = pl.ds(j * BS, BS)
+                total = part[q, here, :].astype(F32) + agg_in[slot_of[q], here, :].astype(F32)
+                part[q, here, :] = total.astype(BF16)
+                cnt[q, j] = cnt[q, j] + cagg_in[slot_of[q], j]
+                for k in inner_out[q, j]:
                     k.start()
 
         def tables(q):
@@ -332,26 +382,27 @@
                     tabc(3, order[q], z, p).wait_recv()
 
         def arrive():
-            for k in edge_out[2]:
-                k.wait_recv()
+            for j in range(per):
+                here = pl.ds(j * BS, BS)
+                for k in edge_out[2, j]:
+                    k.wait_recv()
+                own_sum[here, :] += fin_in[0, here, :].astype(F32)
+                cnt[nz - 1, j] = cnt[nz - 1, j] + cfin_in[0, j]
 
             @pl.when(inner)
             def _():
-                for k in inner_out[1]:
-                    k.wait_recv()
-
-                @pl.loop(0, per)
-                def _(j):
-                    here = pl.ds(pl.multiple_of(j * BS, BS), BS)
+                for j in range(per):
+                    here = pl.ds(j * BS, BS)
+                    for k in inner_out[2, j]:
+                        k.wait_recv()
                     own_sum[here, :] += fin_in[1, here, :].astype(F32)
-
-                cnt[nz - 1] = cnt[nz - 1] + cfin_in[1]
+                    cnt[nz - 1, j] = cnt[nz - 1, j] + cfin_in[1, j]
 
     else:
         direct = []
         for q in range(nz - 1):
-            direct.append(copy(part.at[q], fin_in.at[q], s_sum.at[q], r_fin.at[q], to(g, zq(q), y)))
-            direct.append(copy(cnt.at[q], cfin_in.at[q], s_cnt.at[q], r_cfin.at[q], to(g, zq(q), y)))
+            direct.append(copy(part.at[q], fin_in.at[q], s_sum.at[q, 0], r_fin.at[q, 0], to(g, zq(q), y)))
+            direct.append(copy(cnt.at[q], cfin_in.at[q], s_cnt.at[q, 0], r_cfin.at[q, 0], to(g, zq(q), y)))
 
         def arrive():
             for q in direct:
@@ -361,25 +412,66 @@
         dx, dc = k // 2, k % 2
         return (x + dx) % nx * 2 + (c + dc) % 2
 
-    x_c = {k: copy(xs.at[group(k)], xin.at[k - 1], s_x.at[k], r_x.at[k], to(group(k), z, y)) for k in range(1, G)}
-
-    def finish():
-        arrive()
-        for j in range(per):
-            here = pl.ds(j * BS, BS)
-            total, many = own_sum[here, :], cnt[nz - 1, j]
-            for f in range(1 if cf.line else cf.fins):
-                total += fin_in[f, here, :].astype(F32)
-                many += cfin_in[f, j]
-            many = 1.0 / (jnp.transpose(many)[:, 0:1] + 1.0)
-            fresh = ((total + tab[z, here, :].astype(F32)) * many).astype(BF16)
-            for k in range(G):
-                xs[k, here, :] = fresh[:, k * share : (k + 1) * share]
-        for k in list(range(2, G)) + [1]:
+    def settle(xq, cq, block):
+        fresh_out[pl.ds(start_of(xq, cq), quarter), :] = block.astype(F32)
+
+    if cf.line:
+        side = 2 * share
+        mine, theirs = (pl.ds(pl.multiple_of(k * side, side), side) for k in (x, 1 - x))
+        across, beside = to((1 - x) * 2 + c, z, y), to(x * 2 + 1 - c, z, y)
+        side_c = [
+            [
+                [
+                    copy(x_out.at[k, j], x_in.at[k, j], s_side.at[k, j], r_side.at[k, j], across),
+                    copy((cnt_oth if k else cnt.at[nz - 1]).at[j], cx_in.at[k, j], s_cside.at[k, j], r_cside.at[k, j], across),
+                ]
+                for j in range(per)
+            ]
+            for k in (0, 1)
+        ]
+        x_c = {k: copy(xs.at[(1 - c) * 2 + k], xin.at[k], s_x.at[k], r_x.at[k], beside) for k in (0, 1)}
+
+        def cross(k):
+            total = oth_sum if k else own_sum
+            for j in range(per):
+                here = pl.ds(j * BS, BS)
+                x_out[k, j] = total[here, theirs].astype(BF16)
+                for q in side_c[k][j]:
+                    q.start()
+
+        def finish(k):
+            for j in range(per):
+                for q in side_c[1 - k][j]:
+                    q.wait_recv()
+                here = pl.ds(j * BS, BS)
+                total = oth_sum[here, mine] if k else own_sum[here, mine]
+                old = tab_x[here, mine] if k else tab[z, here, mine]
+                many = (cnt_oth[j] if k else cnt[nz - 1, j]) + cx_in[1 - k, j]
+                many = 1.0 / (jnp.transpose(many)[:, 0:1] + 1.0)
+                total = total + x_in[1 - k, j].astype(F32) + old.astype(F32)
+                fresh = (total * many).astype(BF16)
+                for i in range(2):
+                    xs[i * 2 + k, here, :] = fresh[:, i * share : (i + 1) * share]
             x_c[k].start()
-
-    def settle(gg, block):
-        fresh_out[pl.ds(pl.multiple_of(gg * quarter, quarter), quarter), :] = block.astype(F32)
+            settle((x + k) % 2, c, xs[c * 2 + k])
+
+    else:
+        x_c = {k: copy(xs.at[group(k)], xin.at[k - 1], s_x.at[k], r_x.at[k], to(group(k), z, y)) for k in range(1, G)}
+
+        def finish():
+            arrive()
+            for j in range(per):
+                here = pl.ds(j * BS, BS)
+                total, many = own_sum[here, :], cnt[nz - 1, j]
+                for f in range(cf.fins):
+                    total += fin_in[f, here, :].astype(F32)
+                    many += cfin_in[f, j]
+                many = 1.0 / (jnp.transpose(many)[:, 0:1] + 1.0)
+                fresh = ((total + tab[z, here, :].astype(F32)) * many).astype(BF16)
+                for k in range(G):
+                    xs[k, here, :] = fresh[:, k * share : (k + 1) * share]
+            for k in list(range(2, G)) + [1]:
+                x_c[k].start()
 
     if cf.line:
         pack(0)
@@ -395,21 +487,42 @@
             forward([f_edge], p)
         sums(1)
         lift(1)
-        merge(0)
+        for j in range(per):
+            merge(0, j)
         tables(1)
         dists(1)
+        merge(1, 0)
         sums(2)
         lift(2)
-        merge(1)
-        merge(2)
+        for j in range(1, per):
+            merge(1, j)
+        for j in range(per):
+            merge(2, j)
         tables(0)
         tables(2)
         dists(0)
         dists(2)
-        sums(3)
-        dists(3)
-        finish()
-        late = [1, 0, 2]
+        load_other.wait()
+        near_sums(3, 1)
+        cross(1)
+        near_dists(3, 1)
+        gather(1, 0, TM // 2)
+        gather(0, 0, TM // 2)
+        gather(2, 0, TM // 2)
+        near_sums(3, 0)
+        arrive()
+        cross(0)
+        near_dists(3, 0)
+        gather(1, TM // 2, TM)
+        finish(0)
+        gather(0, TM // 2, TM)
+        gather(3, 0, TM // 2)
+        gather(2, TM // 2, TM)
+        finish(1)
+        gather(3, TM // 2, TM)
+        for k in (0, 1):
+            x_c[k].wait_recv()
+            settle((x + k) % 2, 1 - c, xin[k])
     else:
         for s in range(steps):
             pack(s)
@@ -422,21 +535,23 @@
         for s in range(steps):
             dists(s)
         finish()
-        late = list(range(steps - 1))
-    for s in late + [steps - 1]:
-        gather(s)
-    settle(g, xs[g])
-    for k in range(1, G):
-        x_c[k].wait_recv()
-        dx, dc = k // 2, k % 2
-        settle((x + nx - dx) % nx * 2 + (c + dc) % 2, xin[k - 1])
+        for s in range(steps):
+            gather(s, 0, TM)
+        settle(x, c, xs[g])
+        for k in range(1, G):
+            x_c[k].wait_recv()
+            dx, dc = k // 2, k % 2
+            settle((x + nx - dx) % nx, (c + dc) % 2, xin[k - 1])
 
     for group_c in (pts_c, tgt_c, ret_c, x_c):
         for q in group_c.values():
             q.wait_send()
     if cf.line:
-        for q in own_up + edge_out[0] + edge_out[1] + edge_out[2]:
+        for q in own_up:
             q.wait_send()
+        for group_c in side_c[0] + side_c[1] + list(edge_out.values()):
+            for q in group_c:
+                q.wait_send()
 
         @pl.when(inner)
         def _():
@@ -484,10 +599,17 @@
             vm((steps, tm, MSG, BS), BF16),
             vm((n_grp, quarter, share), BF16),
             vm((n_grp - 1, quarter, share), BF16),
+            vm((quarter, width), BF16),
+            vm((quarter, width), F32),
+            vm((cf.per, 8, BS), F32),
+            vm((2, cf.per, BS, 2 * share), BF16),
+            vm((2, cf.per, BS, 2 * share), BF16),
+            vm((2, cf.per, 8, BS), F32),
             dma((steps, tm)), dma((steps, tm)), dma((steps, tm)), dma((steps, tm)),
             dma((max(5, nz), cf.per)), dma((nz, cf.per)),
-            dma((nz - 1,)), dma((3,)), dma((cf.fins,)), dma((nz - 1,)), dma((3,)), dma((cf.fins,)),
-            dma((steps, tm)), dma((steps, tm)), dma((n_grp,)), dma((n_grp,)), dma((2,)),
+            dma((nz - 1, cf.per)), dma((3, cf.per)), dma((cf.fins, cf.per)), dma((nz - 1, cf.per)), dma((3, cf.per)), dma((cf.fins, cf.per)),
+            dma((steps, tm)), dma((steps, tm)), dma((n_grp,)), dma((n_grp,)),
+            dma((2, cf.per)), dma((2, cf.per)), dma((2, cf.per)), dma((2, cf.per)), dma((3,)),
         ],
         compiler_params=pltpu.CompilerParams(
             collective_id=0, has_side_effects=True, vmem_limit_bytes=58_000_000

time: 139 us -> 131 us (0.942)
  Pallas kernels: 135 us -> 128 us
    pallas_call x1, Pallas kernels: 135 us -> 128 us  [shards(): pl.pallas_call(functools.partial(kernel, cf), out_shape=(vm((npts, BS), B...]
where the time goes in v3:
time: 131 us
  Pallas kernels  128 us (98%)
  local copies, waits for them, and re-layouts  2.29 us (2%)
    pallas_call x1, Pallas kernels, shards(): pl.pallas_call(functools.partial(kernel, cf), out_shape=(vm((npts, BS), B...  128 us

profile of v3, /device:TPU:0, one launch (start us, length us, event | category | flops | bytes accessed | tf_op | source)
XLA Modules:
  0.0 130.7 jit_solution(2303286112956187720)
XLA Ops:
  0.6 127.7 %shard_map.59 = (bf16[2048,256]{1,0:T(8,128)(2,1)S(1)}, f32[2048,256]{1,0:T(8,128)S(1)}) custom-call(s32[1,2048]{1,0:T(1,128)} %bitcast.2, s32[1,2048]{1,0:T(1,128)} %bitcast.3, bf16[2048,1024]{1,0:T(8,128)(2,1)} %points_hbm.1, bf16[2048,1024]{1,0:T(8,128)(2,1)} %cent_hbm.1), custom_call_target="tpu_custom_call" | custom-call | tf_op jit(solution)/shard_map/pallas_call | solution.py:577
  128.4 1.0 copy.8
  129.3 1.3 %copy.9 = f32[2048,256]{1,0:T(8,128)} copy(f32[2048,256]{1,0:T(8,128)S(1)} %get-tuple-element.3) | data formatting | bytes 4194304

commit v4 on v3

--- a/solution.py
+++ b/solution.py
@@ -37,7 +37,7 @@
         self.steps = self.nz * self.per * self.depth // MSG
         self.zs = self.nz // self.steps
         self.nblk = self.zs * self.per
-        self.line = self.nz == 4 and self.nx == 2
+        self.line = (self.nx, self.ny, self.nz) == (2, 2, 4)
         self.fins = 2 if self.line else self.nz - 1
 
 
@@ -105,12 +105,10 @@
     )
     load_points = pltpu.make_async_copy(points_hbm, points, in_sem.at[1])
     load_points.start()
-    load_tab.start()
     if cf.line:
         load_other = pltpu.make_async_copy(
             cent_hbm.at[pl.ds(start_of(1 - x, c), quarter)], tab_x, in_sem.at[2]
         )
-        load_other.start()
 
     barrier = pltpu.get_barrier_semaphore()
     peers = [mate(o) for o in range(1, TM)] + [to(g, (z + k) % nz, y) for k in range(1, nz)]
@@ -159,6 +157,9 @@
         slot_col[here, :] = jnp.transpose(jnp.broadcast_to(slot.astype(F32), (8, step)))
     want_row = jnp.broadcast_to((final_row[...] + 1).astype(F32), (8, npts)).astype(BF16)
     load_points.wait()
+    load_tab.start()
+    if cf.line:
+        load_other.start()
 
     pts_c, tgt_c, ret_c = {}, {}, {}
     for s in range(steps):
@@ -167,12 +168,12 @@
             tgt_c[s, o] = copy(tgt_out.at[s, o], tgt_in.at[s, o], s_tgt.at[s, o], r_tgt.at[s, o], mate(o, s))
             ret_c[s, o] = copy(dist.at[s, o], ret.at[s, o], s_ret.at[s, o], r_ret.at[s, o], back(o, s))
 
-    def tile(s, lo):
+    def tile(s, lo, n=2):
         base = (s * TM + lo) * MSG
-        hot = (lax.broadcasted_iota(I32, (2 * MSG, npts), 0) + base == slot_row[...]).astype(BF16)
+        hot = (lax.broadcasted_iota(I32, (n * MSG, npts), 0) + base == slot_row[...]).astype(BF16)
         pts = jnp.dot(hot, points[...], preferred_element_type=F32).astype(BF16)
         tg = nt(want_row, hot)
-        for i in range(2):
+        for i in range(n):
             o = lo + i
             rows, lanes = pts[i * MSG : (i + 1) * MSG], tg[:, i * MSG : (i + 1) * MSG]
             if o in remote(s):
@@ -182,21 +183,24 @@
                 recv[s, o] = rows
                 tgt_in[s, o] = lanes
 
-    def send(s, lo):
-        for o in (lo, lo + 1):
+    def send(s, lo, n=2):
+        for o in range(lo, lo + n):
             if o in remote(s):
                 tgt_c[s, o].start()
                 pts_c[s, o].start()
 
     def pack(s):
-        for lo in range(TM - 2, -1, -2):
-            if (s, lo) != (0, TM - 2):
+        for lo in ([6, 2, 4, 0] if near(s) else [4, 6, 2, 0]) if cf.line else range(TM - 2, -1, -2):
+            if (s, lo) != (0, first_lo):
                 tile(s, lo)
                 send(s, lo)
 
-    tile(0, TM - 2)
+    first_lo = 4 if cf.line else TM - 2
+    tile(0, first_lo, 1)
     pl.semaphore_wait(barrier, len(peers))
-    send(0, TM - 2)
+    send(0, first_lo, 1)
+    tile(0, first_lo + 1, 1)
+    send(0, first_lo + 1, 1)
 
     load_tab.wait()
     if cf.line:
@@ -518,8 +522,9 @@
         gather(0, TM // 2, TM)
         gather(3, 0, TM // 2)
         gather(2, TM // 2, TM)
+        gather(3, TM - 2, TM)
         finish(1)
-        gather(3, TM // 2, TM)
+        gather(3, TM // 2, TM - 2)
         for k in (0, 1):
             x_c[k].wait_recv()
             settle((x + k) % 2, 1 - c, xin[k])

time: 131 us -> 129 us (0.985)
  Pallas kernels: 128 us -> 126 us
    pallas_call x1, Pallas kernels: 128 us -> 126 us  [shards(): pl.pallas_call(functools.partial(kernel, cf), out_shape=(vm((npts, BS), B...]
where the time goes in v4:
time: 129 us
  Pallas kernels  126 us (98%)
  local copies, waits for them, and re-layouts  2.29 us (2%)
    pallas_call x1, Pallas kernels, shards(): pl.pallas_call(functools.partial(kernel, cf), out_shape=(vm((npts, BS), B...  126 us

profile of v4, /device:TPU:0, one launch (start us, length us, event | category | flops | bytes accessed | tf_op | source)
XLA Modules:
  0.0 128.6 jit_solution(13736737393730520335)
XLA Ops:
  0.6 125.7 %shard_map.59 = (bf16[2048,256]{1,0:T(8,128)(2,1)S(1)}, f32[2048,256]{1,0:T(8,128)S(1)}) custom-call(s32[1,2048]{1,0:T(1,128)} %bitcast.2, s32[1,2048]{1,0:T(1,128)} %bitcast.3, bf16[2048,1024]{1,0:T(8,128)(2,1)} %points_hbm.1, bf16[2048,1024]{1,0:T(8,128)(2,1)} %cent_hbm.1), custom_call_target="tpu_custom_call" | custom-call | tf_op jit(solution)/shard_map/pallas_call | solution.py:582
  126.3 1.0 copy.8
  127.3 1.3 %copy.9 = f32[2048,256]{1,0:T(8,128)} copy(f32[2048,256]{1,0:T(8,128)S(1)} %get-tuple-element.3) | data formatting | bytes 4194304
